TPU v7x, 8 devices: a whole 2x2x1 slice. The times are simulated.
8 devices in a mesh: rhs: 1 (over z), mz: 2 (over y), my: 2 (over x), mx: 2 (over core).
Axes of the slice: x: 2, y: 2, z: 1, core: 2. Of those that a mesh axis runs over, the one named last changes fastest.
Arguments:
- x_vol: bfloat16 [128, 128, 128, 64], P('mx', 'my', 'mz', 'rhs')
- fac_a1: bfloat16 [32, 128], replicated
- fac_a2: bfloat16 [32, 128], replicated
- fac_a3: bfloat16 [32, 128], replicated
- diag_d: float32 [32, 32, 32], P('mx', 'my', 'mz')
- fac_b1: bfloat16 [128, 32], replicated
- fac_b2: bfloat16 [128, 32], replicated
- fac_b3: bfloat16 [128, 32], replicated
Outputs:
- output: float32 [128, 128, 128, 64], P('mx', 'my', 'mz', 'rhs')
All inputs are finite; a program needn't handle non-finite values.
Results may differ from a plain program's by a relative error of at most 0.0125944.
Values are sent between devices in bfloat16 or wider.
A program may use at most 1 GiB of HBM per device.

v0:
```python
import jax
import jax.numpy as jnp
from jax import lax
from jax.sharding import PartitionSpec as P


def solution(mesh):
    vol_spec = P("mx", "my", "mz", "rhs")
    core_spec = P("mx", "my", "mz")
    full_spec = P()

    def local_operator(x_blk, fac_a1, fac_a2, fac_a3, diag_blk, fac_b1, fac_b2, fac_b3):
        rows_one = x_blk.shape[0]
        rows_two = x_blk.shape[1]
        rows_three = x_blk.shape[2]
        pos_one = lax.axis_index("mx")
        pos_two = lax.axis_index("my")
        pos_three = lax.axis_index("mz")
        a1_cols = lax.dynamic_slice_in_dim(fac_a1, pos_one * rows_one, rows_one, axis=1)
        part_one = jnp.einsum("ia,ajkr->ijkr", a1_cols, x_blk, preferred_element_type=jnp.float32)
        u_one = lax.psum_scatter(part_one, "mx", scatter_dimension=0, tiled=True).astype(jnp.bfloat16)
        a2_cols = lax.dynamic_slice_in_dim(fac_a2, pos_two * rows_two, rows_two, axis=1)
        part_two = jnp.einsum("jb,ibkr->ijkr", a2_cols, u_one, preferred_element_type=jnp.float32)
        u_two = lax.psum_scatter(part_two, "my", scatter_dimension=1, tiled=True).astype(jnp.bfloat16)
        a3_cols = lax.dynamic_slice_in_dim(fac_a3, pos_three * rows_three, rows_three, axis=1)
        part_three = jnp.einsum("kc,ijcr->ijkr", a3_cols, u_two, preferred_element_type=jnp.float32)
        u_three = lax.psum_scatter(part_three, "mz", scatter_dimension=2, tiled=True).astype(jnp.bfloat16)
        w_core = (diag_blk[:, :, :, None] * u_three.astype(jnp.float32)).astype(jnp.bfloat16)
        w_gathered = lax.all_gather(w_core, "mz", axis=2, tiled=True)
        b3_rows = lax.dynamic_slice_in_dim(fac_b3, pos_three * rows_three, rows_three, axis=0)
        v_three = jnp.einsum("kc,ijcr->ijkr", b3_rows, w_gathered, preferred_element_type=jnp.float32).astype(jnp.bfloat16)
        v3_gathered = lax.all_gather(v_three, "my", axis=1, tiled=True)
        b2_rows = lax.dynamic_slice_in_dim(fac_b2, pos_two * rows_two, rows_two, axis=0)
        v_two = jnp.einsum("jb,ibkr->ijkr", b2_rows, v3_gathered, preferred_element_type=jnp.float32).astype(jnp.bfloat16)
        v2_gathered = lax.all_gather(v_two, "mx", axis=0, tiled=True)
        b1_rows = lax.dynamic_slice_in_dim(fac_b1, pos_one * rows_one, rows_one, axis=0)
        return jnp.einsum("ia,ajkr->ijkr", b1_rows, v2_gathered, preferred_element_type=jnp.float32)

    return jax.shard_map(local_operator, mesh=mesh, in_specs=(vol_spec, full_spec, full_spec, full_spec, core_spec, full_spec, full_spec, full_spec), out_specs=vol_spec, check_vma=False)
```

profile of v0, /device:TPU:0, one launch (start us, length us, event | category | flops | bytes accessed | tf_op | source)
XLA Modules:
  0.0 887.0 jit_solution(13686348107160295458)
XLA Ops:
  6.5 69.0 %fusion = f32[32,64,64,64]{3,0,2,1:T(8,128)} fusion(bf16[64,64,64,64]{3,2,1,0:T(8,128)(2,1)} %param.8, bf16[32,128]{1,0:T(8,128)(2,1)} %param.9, s32[]{:T(128)S(6)} %select_n.12), kind=kOutput, calls=%fused_computation | convolution fusion | flops 1073741824 | bytes 67117056 | tf_op jit(solution)/shard_map/ia,ajkr->ijkr/dot_general | solution.py:20
  75.6 45.2 %copy.13 = f32[32,64,64,64]{3,2,1,0:T(8,128)} copy(f32[32,64,64,64]{3,0,2,1:T(8,128)} %fusion) | data formatting | bytes 67108864 | tf_op jit(solution)/shard_map/ia,ajkr->ijkr/dot_general | solution.py:20
  120.8 0.2 reduce-scatter.6.cloned.1.call-start
  121.0 76.7 %reduce-scatter.4.cloned.1.call-done = f32[16,64,64,64]{3,2,1,0:T(8,128)} async-done(((f32[32,64,64,64]{3,2,1,0:T(8,128)}), f32[16,64,64,64]{3,2,1,0:T(8,128)}) %reduce-scatter.4.cloned.1.call-update) | async-done | bytes 16777232 | tf_op jit(solution)/shard_map/reduce_scatter | solution.py:21
  197.8 18.2 %convert_element_type.27 = bf16[16,64,64,64]{3,2,1,0:T(8,128)(2,1)} convert(f32[16,64,64,64]{3,2,1,0:T(8,128)} %reduce-scatter.4.cloned.1.call-done) | non-fusion elementwise | flops 4194304 | bytes 25165824 | tf_op jit(solution)/shard_map/convert_element_type | solution.py:21
  215.9 23.2 %fusion.2 = f32[16,64,64,32]{2,3,1,0:T(8,128)} fusion(bf16[16,64,64,64]{3,2,1,0:T(8,128)(2,1)} %convert_element_type.27, bf16[32,128]{1,0:T(8,128)(2,1)S(1)} %copy-done.3, s32[]{:T(128)S(6)} %select_n.13), kind=kOutput, calls=%fused_computation.3 | convolution fusion | flops 268435456 | bytes 16785412 | tf_op jit(solution)/shard_map/jb,ibkr->ijkr/dot_general | solution.py:23
  239.1 14.2 %copy.34 = f32[16,64,64,32]{2,1,0,3:T(8,128)} copy(f32[16,64,64,32]{2,3,1,0:T(8,128)} %fusion.2) | data formatting | bytes 16777216 | tf_op jit(solution)/shard_map/jb,ibkr->ijkr/dot_general | solution.py:23
  253.3 0.0 reduce-scatter.8.cloned.1.call-start
  253.4 187.6 %reduce-scatter.6.cloned.1.call-done = f32[16,16,64,64]{3,2,0,1:T(8,128)} async-done(((f32[16,32,64,64]{3,2,0,1:T(8,128)}), f32[16,16,64,64]{3,2,0,1:T(8,128)}) %reduce-scatter.6.cloned.1.call-update) | async-done | bytes 4194320 | tf_op jit(solution)/shard_map/reduce_scatter | solution.py:24
  440.9 6.2 fusion.6
  447.1 0.0 all-gather.4.cloned.1.call-start
  447.2 51.6 %reduce-scatter.8.cloned.1.call-done = f32[16,16,16,64]{3,2,1,0:T(8,128)} async-done(((f32[16,16,32,64]{3,2,1,0:T(8,128)}), f32[16,16,16,64]{3,2,1,0:T(8,128)}) %reduce-scatter.8.cloned.1.call-update) | async-done | bytes 1048592 | tf_op jit(solution)/shard_map/reduce_scatter | solution.py:27
  498.8 2.7 multiply_convert_fusion
  501.5 0.0 all-gather.6.cloned.1.call-start
  501.5 30.2 %all-gather.4.cloned.1.call-done = bf16[16,16,32,64]{3,2,1,0:T(8,128)(2,1)} async-done(((bf16[16,16,16,64]{3,2,1,0:T(8,128)(2,1)}), bf16[16,16,32,64]{3,2,1,0:T(8,128)(2,1)}) %all-gather.4.cloned.1.call-update) | async-done | bytes 1048592 | tf_op jit(solution)/shard_map/all_gather | solution.py:29
  531.8 4.9 convert_bitcast_fusion.1
  536.7 0.0 all-gather.8.cloned.1.call-start
  536.8 102.4 %all-gather.6.cloned.1.call-done = bf16[16,32,64,64]{2,3,1,0:T(8,128)(2,1)} async-done(((bf16[16,16,64,64]{2,3,1,0:T(8,128)(2,1)}), bf16[16,32,64,64]{2,3,1,0:T(8,128)(2,1)}) %all-gather.6.cloned.1.call-update) | async-done | bytes 4194320 | tf_op jit(solution)/shard_map/all_gather | solution.py:32
  639.2 13.1 %copy.20 = bf16[16,32,64,64]{3,1,2,0:T(8,128)(2,1)} copy(bf16[16,32,64,64]{2,3,1,0:T(8,128)(2,1)} %all-gather.6.cloned.1.call-done) | data formatting | bytes 8388608 | tf_op jit(solution)/shard_map/all_gather | solution.py:32
  652.2 10.8 %fusion.9 = bf16[16,64,64,64]{3,2,1,0:T(8,128)(2,1)} fusion(bf16[16,32,64,64]{3,1,2,0:T(8,128)(2,1)} %copy.20, bf16[128,32]{0,1:T(8,128)(2,1)S(1)} %copy-done.5, s32[]{:T(128)S(6)} %select_n.13), kind=kOutput, calls=%fused_computation.11 | convolution fusion | flops 268435456 | bytes 12591108 | tf_op jit(solution)/shard_map/jb,ibkr->ijkr/dot_general | solution.py:34
  663.0 23.4 %copy.22 = bf16[16,64,64,64]{2,0,1,3:T(8,128)(2,1)} copy(bf16[16,64,64,64]{3,2,1,0:T(8,128)(2,1)} %fusion.9) | data formatting | bytes 16777216 | tf_op jit(solution)/shard_map/jb,ibkr->ijkr/dot_general | solution.py:34
  686.4 48.2 %all-gather.8.cloned.1.call-done = bf16[32,64,64,64]{3,0,2,1:T(8,128)(2,1)} async-done(((bf16[16,64,64,64]{3,0,2,1:T(8,128)(2,1)}), bf16[32,64,64,64]{3,0,2,1:T(8,128)(2,1)}) %all-gather.8.cloned.1.call-update) | async-done | bytes 16777232 | tf_op jit(solution)/shard_map/all_gather | solution.py:35
  734.6 56.7 %fusion.15 = f32[64,64,64,64]{3,0,2,1:T(8,128)} fusion(bf16[32,64,64,64]{3,0,2,1:T(8,128)(2,1)} %all-gather.8.cloned.1.call-done, bf16[128,32]{0,1:T(8,128)(2,1)S(1)} %copy-done, s32[]{:T(128)S(6)} %select_n.12), kind=kOutput, calls=%fused_computation.17 | convolution fusion | flops 1073741824 | bytes 83894272 | tf_op jit(solution)/shard_map/ia,ajkr->ijkr/dot_general | solution.py:37
  791.3 88.8 %copy.10 = f32[64,64,64,64]{3,2,1,0:T(8,128)} copy(f32[64,64,64,64]{3,0,2,1:T(8,128)} %fusion.15) | data formatting | bytes 134217728 | tf_op jit(solution)/shard_map/ia,ajkr->ijkr/dot_general | solution.py:37
  (21 shorter events, 0.1 us)
Async XLA Ops:
  6.5 728.1 %copy-start = (bf16[128,32]{0,1:T(8,128)(2,1)S(1)}, bf16[128,32]{0,1:T(8,128)(2,1)}, u32[]{:S(2)}) copy-start(bf16[128,32]{0,1:T(8,128)(2,1)} %param.13) | copy-start | bytes 24580
  6.5 191.2 %reduce-scatter.4.cloned.1.call-start = ((), (), s32[]{:S(2)}) async-start(), calls=%async_computation.3 | async-start | bytes 100663296 | tf_op jit(solution)/shard_map/reduce_scatter | solution.py:21
  120.8 320.1 %reduce-scatter.6.cloned.1.call-start = ((), (), s32[]{:S(2)}) async-start(), calls=%async_computation.4 | async-start | bytes 25165824 | tf_op jit(solution)/shard_map/reduce_scatter | solution.py:24
  121.0 94.9 %copy-start.3 = (bf16[32,128]{1,0:T(8,128)(2,1)S(1)}, bf16[32,128]{1,0:T(8,128)(2,1)}, u32[]{:S(2)}) copy-start(bf16[32,128]{1,0:T(8,128)(2,1)} %param.10) | copy-start | bytes 24580
  253.3 187.6 %copy-start.6 = (bf16[32,128]{1,0:T(8,128)(2,1)S(1)}, bf16[32,128]{1,0:T(8,128)(2,1)}, u32[]{:S(2)}) copy-start(bf16[32,128]{1,0:T(8,128)(2,1)} %param.11) | copy-start | bytes 24580
  253.3 245.5 %copy-start.2 = (f32[16,16,16]{2,1,0:T(8,128)S(1)}, f32[16,16,16]{2,1,0:T(8,128)}, u32[]{:S(2)}) copy-start(f32[16,16,16]{2,1,0:T(8,128)} %param.12) | copy-start | bytes 49156
  253.3 278.5 %copy-start.4 = (bf16[128,32]{0,1:T(8,128)(2,1)S(1)}, bf16[128,32]{0,1:T(8,128)(2,1)}, u32[]{:S(2)}) copy-start(bf16[128,32]{0,1:T(8,128)(2,1)} %param.15) | copy-start | bytes 24580
  253.3 245.4 %reduce-scatter.8.cloned.1.call-start = ((), (), s32[]{:S(2)}) async-start(), calls=%async_computation.5 | async-start | bytes 6291456 | tf_op jit(solution)/shard_map/reduce_scatter | solution.py:27
  447.1 205.1 %copy-start.5 = (bf16[128,32]{0,1:T(8,128)(2,1)S(1)}, bf16[128,32]{0,1:T(8,128)(2,1)}, u32[]{:S(2)}) copy-start(bf16[128,32]{0,1:T(8,128)(2,1)} %param.14) | copy-start | bytes 24580
  447.1 84.6 %all-gather.4.cloned.1.call-start = ((), (), s32[]{:S(2)}) async-start(), calls=%async_computation.6 | async-start | bytes 3145728 | tf_op jit(solution)/shard_map/all_gather | solution.py:29
  501.5 137.7 %all-gather.6.cloned.1.call-start = ((), (), s32[]{:S(2)}) async-start(), calls=%async_computation.7 | async-start | bytes 12582912 | tf_op jit(solution)/shard_map/all_gather | solution.py:32
  536.7 197.9 %all-gather.8.cloned.1.call-start = ((), (), s32[]{:S(2)}) async-start(), calls=%async_computation.8 | async-start | bytes 50331648 | tf_op jit(solution)/shard_map/all_gather | solution.py:35
  791.3 88.8 %copy-start.1 = (bf16[128,32]{0,1:T(8,128)(2,1)S(1)}, bf16[128,32]{0,1:T(8,128)(2,1)}, u32[]{:S(2)}) copy-start(bf16[128,32]{0,1:T(8,128)(2,1)} %param.13) | copy-start | bytes 24580
Sparse Core Ops, SparseCore 0:
  120.9 76.8 reduce-scatter.3
  253.4 187.4 reduce-scatter.5
  447.2 51.4 reduce-scatter.7
  501.6 30.1 all-gather.3
  536.9 102.2 all-gather.5
  686.5 48.0 all-gather.7
where the time goes:
time: 888 us; the launch traced here: 887 us
  waiting for transfers between devices  497 us (56%)
  local copies, waits for them, and re-layouts  185 us (21%)
  matrix products  171 us (19%)
  other arithmetic  20.9 us (2%)
  between operations  13.5 us (2%)
    reduce_scatter x1, waiting for transfers between devices, local_operator(): lax.psum_scatter(part_two, 'my', scatter_dimension=1, tiled=True)  188 us
    all_gather x1, waiting for transfers between devices, local_operator(): v3_gathered = lax.all_gather(v_three, 'my', axis=1, tiled=True)  102 us
    dot_general x1, local copies, waits for them, and re-layouts, local_operator(): jnp.einsum('ia,ajkr->ijkr', b1_rows, v2_gathered, preferred_element_type=...  88.8 us
    reduce_scatter x1, waiting for transfers between devices, local_operator(): lax.psum_scatter(part_one, 'mx', scatter_dimension=0, tiled=True)  76.7 us
    dot_general x1, matrix products, local_operator(): jnp.einsum('ia,ajkr->ijkr', a1_cols, x_blk, preferred_element_type=jnp.fl...  69 us
    dot_general x1, matrix products, local_operator(): jnp.einsum('ia,ajkr->ijkr', b1_rows, v2_gathered, preferred_element_type=...  56.7 us
    reduce_scatter x1, waiting for transfers between devices, local_operator(): lax.psum_scatter(part_three, 'mz', scatter_dimension=2, tiled=True)  51.6 us
    all_gather x1, waiting for transfers between devices, local_operator(): v2_gathered = lax.all_gather(v_two, 'mx', axis=0, tiled=True)  48.2 us
  transfers between devices with their start and end apart: 6, of which 6 were waited for; matrix products, arithmetic and copies ran while one was open for 0% of the time, Pallas kernels for 0%

commit v1 on v0

v1 whole, which is shorter than its diff:
```python
import jax
import jax.numpy as jnp
from jax import lax
from jax.experimental import pallas as pl
from jax.experimental.pallas import tpu as pltpu
from jax.sharding import PartitionSpec as P

F32 = jnp.float32
BF16 = jnp.bfloat16
MESH = pl.DeviceIdType.MESH
N = 64
M = 32
L = 128
T = 16
S = 8
TWO = 2
QUART = 4
H = M // TWO
RING = 8
AHEAD = 4
NEAR = 4
STEPS = N // TWO
EARLY = 10
A, B, C, D, E = range(5)
SIZES = (4, 6, 3, 2, 1)
STARTS = (0, 4, 10, 13, 15)
CHUNKS = (0, 0, 4, 2, 1)
GROUPS = range(len(SIZES))
OTHERS = range(1, QUART)
DEVICES = range(1, S)
KINDS = 7
LIMIT = 62 * 1024 * 1024


def dot(a, b):
    return jnp.dot(a, b, preferred_element_type=F32)


def dot_t(a, b):
    return lax.dot_general(a, b, (((0,), (0,)), ((), ())), preferred_element_type=F32)


def iota(shape, axis):
    return lax.broadcasted_iota(jnp.int32, shape, axis)


def ones_where(cond):
    return jnp.where(cond, 1.0, 0.0).astype(BF16)


def fill(out_ref, mat, row_of, col_of, keep, product=dot):
    rows, cols = out_ref.shape
    depth = mat.shape[1] if product is dot else mat.shape[0]
    wide = product(mat, ones_where(iota((depth, cols), 0) == col_of(iota((depth, cols), 1)))).astype(BF16)
    for r0 in range(0, rows, L):
        p = iota((L, wide.shape[0]), 0) + r0
        block = dot(ones_where(iota((L, wide.shape[0]), 1) == row_of(p)), wide)
        same = keep(iota((L, cols), 0) + r0, iota((L, cols), 1))
        out_ref[r0:r0 + L, :] = jnp.where(same, block, 0.0).astype(BF16)


def alike(n):
    return lambda p, q: lax.rem(p, n) == lax.rem(q, n)


def compress_body(x_hbm, a1_ref, a2_ref, a3_ref, b2_ref, b3_ref, d_ref, v2_out,
                  xl, xr, u1o, u1s, u1r, k1o, k1r, k2o, k2r, k3, l3, l2, u2s, u2b, wbuf, dall, v3, v2s,
                  near_sem, xs_sem, xr_sem, credit, us_sem, ur_sem, gs_sem, gr_sem,
                  vs_sem, vr_sem, ws_sem, wr_sem, ds_sem, dr_sem, out_sem):
    c = lax.axis_index("mx")
    y = lax.axis_index("my")
    z = lax.axis_index("mz")
    oc, oy, oz = 1 - c, 1 - y, 1 - z

    def flip(rel):
        return (lax.rem(c + rel // QUART, TWO), lax.rem(y + rel // TWO % TWO, TWO), lax.rem(z + rel % TWO, TWO))

    def beside(rel):
        return (lax.rem(c + rel // TWO, TWO), y, lax.rem(z + rel % TWO, TWO))

    def ids(dev):
        return dict(zip(("mx", "my", "mz"), dev))

    def send(src, dst, s_sem, r_sem, dev):
        return pltpu.make_async_remote_copy(src, dst, s_sem, r_sem, device_id=ids(dev), device_id_type=MESH)

    peer, in_x, in_y = (oc, y, z), (c, oy, z), (c, y, oz)

    barrier = pltpu.get_barrier_semaphore()
    for rel in DEVICES:
        pl.semaphore_signal(barrier, inc=1, device_id=ids(flip(rel)), device_id_type=MESH)
    pl.semaphore_wait(barrier, len(DEVICES))

    def half_of(core, t):
        return x_hbm.at[:, pl.ds(TWO * t, TWO), pl.ds(core * M, M), :]

    def near(t):
        slot = lax.rem(t, NEAR)
        return pltpu.make_async_copy(half_of(c, t), xl.at[slot], near_sem.at[slot])

    def cross(t):
        slot = lax.rem(t, RING)
        return send(half_of(oc, t), xr.at[slot], xs_sem.at[slot], xr_sem.at[slot], peer)

    for t in range(AHEAD):
        cross(t).start()
    for t in range(NEAR - 1):
        near(t).start()

    def slot_of(dev):
        return QUART * dev[0] + TWO * dev[1] + dev[2]

    my_slot = slot_of((c, y, z))

    def diag(rel):
        return send(d_ref, dall.at[my_slot], ds_sem.at[rel - 1], dr_sem.at[rel - 1], flip(rel))

    for rel in DEVICES:
        diag(rel).start()
    dall[my_slot] = d_ref[...]

    def rows_one(p):
        return lax.rem(p // T + H * y, M)

    fill(k1o, a1_ref[...], rows_one, lambda q: c * N + q // T, alike(T))
    fill(k1r, a1_ref[...], rows_one, lambda q: oc * N + q // T, alike(T))

    def pack(ref, slot):
        parts = [jnp.concatenate([ref[slot, :, s, 0:T, :], ref[slot, :, s, T:M, :]], axis=-1).reshape(N * T, L)
                 for s in range(TWO)]
        return jnp.concatenate(parts, axis=1)

    def early(t):
        part = (pl.ds(TWO * t, TWO), pl.ds(0, EARLY * T))
        return send(u1s.at[part], u1r.at[part], us_sem.at[t], ur_sem.at[t], in_x)

    def late(g, n):
        span = N // CHUNKS[g]
        part = (pl.ds(span * n, span), pl.ds(STARTS[g] * T, SIZES[g] * T))
        return send(u1s.at[part], u1r.at[part], gs_sem.at[g, n], gr_sem.at[g, n], in_x)

    @pl.loop(0, STEPS)
    def _(t):
        @pl.when(t + NEAR - 1 < STEPS)
        def _():
            near(t + NEAR - 1).start()

        @pl.when(t >= 1)
        def _():
            early(t - 1).start()

        near(t).wait()
        cross(t).wait_recv()
        acc = dot(k1o[...], pack(xl, lax.rem(t, NEAR))) + dot(k1r[...], pack(xr, lax.rem(t, RING)))
        u1 = acc.astype(BF16)
        for s in range(TWO):
            u1o[TWO * t + s] = u1[:H * T, s * L:(s + 1) * L]
            u1s[TWO * t + s] = u1[H * T:, s * L:(s + 1) * L]

        @pl.when(t < STEPS - RING)
        def _():
            pl.semaphore_signal(credit, inc=1, device_id=ids(peer), device_id_type=MESH)

        @pl.when(t + AHEAD >= RING)
        def _():
            cross(t + AHEAD - RING).wait_send()

        @pl.when((t + AHEAD >= RING) & (t + AHEAD < STEPS))
        def _():
            pl.semaphore_wait(credit, 1)

        @pl.when(t + AHEAD < STEPS)
        def _():
            cross(t + AHEAD).start()

    def depart(g):
        for n in range(CHUNKS[g]):
            late(g, n).start()

    early(STEPS - 1).start()
    depart(C)
    for t in range(STEPS - RING + AHEAD, STEPS):
        cross(t).wait_send()

    fill(k2o, a2_ref[...], lambda p: p // T, lambda q: y * N + q // T, alike(T))
    fill(k2r, a2_ref[...], lambda p: p // T, lambda q: oy * N + q // T, alike(T))
    q = iota((L, N), 1)
    k_first = lax.rem(z + q // T % TWO, TWO) * N + lax.rem(c + q // M, TWO) * M + lax.rem(q, T)
    for half in range(TWO):
        sel = ones_where(iota((L, N), 0) == k_first + T * half)
        k3[half * M:(half + 1) * M, :] = dot(a3_ref[...], sel).astype(BF16)
    fill(l2, b2_ref[...], lambda p: y * N + p // S, lambda q: q // S, alike(S), dot_t)
    fill(l3, b3_ref[...], lambda p: z * N + p // L * T + lax.rem(p, T), lambda q: lax.rem(q, M),
         lambda p, q: lax.rem(p, L) // T == q // M, dot_t)

    def second(i, width):
        def side(ref):
            return jnp.concatenate(
                [ref[:, pl.ds(pl.multiple_of((i + s) * T, T), T), :].reshape(N * T, L) for s in range(width)], axis=1)

        out = dot(k2o[...], side(u1o)) + dot(k2r[...], side(u1r))
        for s in range(width):
            u2s[i + s] = out[:, s * L:(s + 1) * L].astype(BF16)

    def quarter(dev):
        return TWO * dev[0] + dev[2]

    mine = quarter((c, y, z))

    def inner(g, rel):
        dev = beside(rel)
        i_span = pl.ds(STARTS[g], SIZES[g])
        return send(u2s.at[i_span, pl.ds(quarter(dev) * L, L)], u2b.at[rel - 1, i_span],
                    vs_sem.at[g, rel], vr_sem.at[g, rel], dev)

    def all_second(g):
        if SIZES[g] >= TWO:
            @pl.loop(0, SIZES[g] // TWO)
            def _(n):
                second(STARTS[g] + TWO * n, TWO)
        if SIZES[g] % TWO:
            second(STARTS[g] + SIZES[g] - 1, 1)
        for rel in (1, QUART - 1, TWO):
            inner(g, rel).start()

    low = iota((M, L), 1) < N
    lane = iota((M, TWO * L), 1)

    def third(g):
        for rel in OTHERS:
            inner(g, rel).wait_recv()
        base = slot_of((y, c, 0))
        d = jnp.concatenate([dall[base], dall[base + 1]], axis=0)

        @pl.loop(0, SIZES[g] * QUART, unroll=QUART)
        def _(n):
            i = STARTS[g] + n // QUART
            jl = lax.rem(n, QUART)

            def column(s):
                row = pl.multiple_of((TWO * jl + s) * T, T)
                own = u2s[i, pl.ds(pl.multiple_of(mine * L + row, T), T), :]
                return jnp.concatenate([own] + [u2b[rel - 1, i, pl.ds(row, T), :] for rel in OTHERS], axis=0)

            out = dot(k3[...], jnp.concatenate([column(0), column(1)], axis=1))
            first, other = out[:M], out[M:]
            u3 = jnp.where(low, first[:, :L] + pltpu.roll(other[:, :L], N, 1),
                           pltpu.roll(first[:, L:], N, 1) + other[:, L:])
            at = i * T + S * z + TWO * jl
            even = jnp.sum(jnp.where(lane == at, d, 0.0), axis=1, keepdims=True)
            odd = jnp.sum(jnp.where(lane == at + 1, d, 0.0), axis=1, keepdims=True)
            w = jnp.where(low, even, odd) * u3.astype(BF16).astype(F32)
            wbuf[y * H + i, mine * QUART + jl] = w.astype(BF16)

    def share(g, kind, owner, dev):
        at = (pl.ds(owner[1] * H + STARTS[g], SIZES[g]), pl.ds(quarter(owner) * QUART, QUART))
        return send(wbuf.at[at], wbuf.at[at], ws_sem.at[g, kind], wr_sem.at[g, kind], dev)

    OWN_X, OWN_Y, OWN_P, X_Y, X_P, Y_P, D_P = range(KINDS)
    diagonal = (c, oy, oz)

    def gather_first(g):
        for kind, dev in ((OWN_X, in_x), (OWN_Y, in_y), (OWN_P, peer)):
            share(g, kind, (c, y, z), dev).start()

    def gather_rest(g):
        share(g, OWN_X, in_x, in_x).wait_recv()
        share(g, X_Y, in_x, in_y).start()
        share(g, X_P, in_x, peer).start()
        share(g, OWN_Y, in_y, in_y).wait_recv()
        share(g, Y_P, in_y, peer).start()
        share(g, X_Y, diagonal, in_y).wait_recv()
        share(g, D_P, diagonal, peer).start()

    def gather_end(g):
        for kind, owner in ((OWN_P, (c, y, z)), (X_P, in_x), (Y_P, in_y), (D_P, diagonal)):
            share(g, kind, (oc,) + owner[1:], peer).wait_recv()

    low_v = iota((QUART, S, S, L), TWO + 1) < N

    def out_copy(p):
        slot = lax.rem(p, TWO)
        return pltpu.make_async_copy(
            v2s.at[slot], v2_out.at[:, :, pl.ds(pl.multiple_of(p * T, T), T), :], out_sem.at[slot])

    def middle(p):
        @pl.when(p >= TWO)
        def _():
            out_copy(p - TWO).wait()

        slot = lax.rem(p, TWO)
        for jo in range(TWO):
            rhs = jnp.concatenate(
                [wbuf[p + H * s, jo * S:(jo + 1) * S].reshape(TWO * L, L) for s in range(TWO)], axis=1)
            out = dot(l3[...], rhs)
            for s in range(TWO):
                o = out[:, s * L:(s + 1) * L].reshape(QUART, S, TWO, S, L)
                t0, t1 = o[:, :, 0], o[:, :, 1]
                even = jnp.where(low_v, t0, pltpu.roll(t1, N, TWO + 1))
                odd = jnp.where(low_v, pltpu.roll(t0, N, TWO + 1), t1)
                both = jnp.concatenate([even, odd], axis=TWO).astype(BF16)
                v3[:, s, jo * L:(jo + 1) * L, :] = both.reshape(QUART, L, L)
        for kb in range(QUART):
            out = dot(l2[...], jnp.concatenate([v3[kb, 0], v3[kb, 1]], axis=1))
            pair = jnp.concatenate([out[:, :L].reshape(N, S, L), out[:, L:].reshape(N, S, L)], axis=1)
            v2s[slot, kb] = pair.astype(BF16)
        out_copy(p).start()

    def all_middle(g):
        @pl.loop(STARTS[g], STARTS[g] + SIZES[g])
        def _(p):
            middle(p)

    def arrived(g):
        for n in range(CHUNKS[g]):
            late(g, n).wait_recv()

    @pl.loop(0, STEPS)
    def _(t):
        early(t).wait_recv()

    for rel in DEVICES:
        diag(rel).wait_recv()
    all_second(A)
    all_second(B)
    third(A)
    gather_first(A)
    depart(D)
    third(B)
    gather_first(B)
    arrived(C)
    all_second(C)
    gather_rest(A)
    third(C)
    gather_first(C)
    depart(E)
    gather_end(A)
    all_middle(A)
    arrived(D)
    all_second(D)
    gather_rest(B)
    third(D)
    gather_first(D)
    gather_rest(C)
    gather_end(B)
    all_middle(B)
    arrived(E)
    all_second(E)
    gather_end(C)
    all_middle(C)
    third(E)
    gather_first(E)
    gather_rest(D)
    gather_end(D)
    all_middle(D)
    gather_rest(E)
    gather_end(E)
    all_middle(E)

    @pl.loop(0, STEPS)
    def _(t):
        early(t).wait_send()

    for rel in DEVICES:
        diag(rel).wait_send()
    for g in GROUPS:
        for n in range(CHUNKS[g]):
            late(g, n).wait_send()
        for rel in OTHERS:
            inner(g, rel).wait_send()
        for kind in range(KINDS):
            share(g, kind, (c, y, z), peer).wait_send()
    out_copy(H - TWO).wait()
    out_copy(H - 1).wait()


def compress(x, a1, a2, a3, b2_t, b3_t, d):
    vmem = pl.BlockSpec(memory_space=pltpu.VMEM)
    hbm = pl.BlockSpec(memory_space=pl.ANY)
    dma = pltpu.SemaphoreType.DMA
    d_flat = d.transpose(2, 0, 1).reshape(H, H * H)
    u1 = pltpu.VMEM((N, H * T, L), BF16)
    spread = pltpu.VMEM((M * T, N * T), BF16)
    groups = len(SIZES)
    return pl.pallas_call(
        compress_body,
        out_shape=jax.ShapeDtypeStruct((QUART, N, M * S, L), BF16),
        in_specs=[hbm] + [vmem] * 6,
        out_specs=hbm,
        scratch_shapes=[
            pltpu.VMEM((NEAR, N, TWO, M, N), BF16), pltpu.VMEM((RING, N, TWO, M, N), BF16), u1, u1, u1,
            spread, spread, spread, spread, pltpu.VMEM((N, N), BF16),
            pltpu.VMEM((M * T, M * S), BF16), pltpu.VMEM((N * S, M * S), BF16),
            pltpu.VMEM((H, M * T, L), BF16), pltpu.VMEM((len(OTHERS), H, L, L), BF16),
            pltpu.VMEM((M, H, M, L), BF16), pltpu.VMEM((S, H, H * H), F32),
            pltpu.VMEM((QUART, TWO, M * S, L), BF16), pltpu.VMEM((TWO, QUART, N, T, L), BF16),
            dma((NEAR,)), dma((RING,)), dma((RING,)), pltpu.SemaphoreType.REGULAR,
            dma((STEPS,)), dma((STEPS,)), dma((groups, QUART)), dma((groups, QUART)),
            dma((groups, QUART)), dma((groups, QUART)), dma((groups, KINDS)), dma((groups, KINDS)),
            dma((KINDS,)), dma((KINDS,)), dma((TWO,)),
        ],
        compiler_params=pltpu.CompilerParams(collective_id=0, has_side_effects=True, vmem_limit_bytes=LIMIT),
        name="compress",
    )(x, a1, a2, a3, b2_t, b3_t, d_flat)


def expand_body(v2_ref, b1_ref, z_ref, l1):
    @pl.when((pl.program_id(0) == 0) & (pl.program_id(1) == 0))
    def _():
        c = lax.axis_index("mx")
        fill(l1, b1_ref[...], lambda p: c * N + p // S, lambda q: lax.rem(q // S, TWO) * H + q // T, alike(S), dot_t)

    for j in range(0, z_ref.shape[1], TWO):
        out = dot(l1[...], jnp.concatenate([v2_ref[0, j], v2_ref[0, j + 1]], axis=1))
        for s in range(TWO):
            o = out[:, s * L:(s + 1) * L].reshape(N, S, L)
            z_ref[:, j + s, :S, :] = o[:, :, :N]
            z_ref[:, j + s, S:, :] = pltpu.roll(o, N, TWO)[:, :, :N]


def expand(v2, b1_t):
    return pl.pallas_call(
        expand_body,
        grid=(QUART, N // S),
        out_shape=jax.ShapeDtypeStruct((N, N, N, N), F32),
        in_specs=[pl.BlockSpec((1, S, M * S, L), lambda kb, jb: (kb, jb, 0, 0)),
                  pl.BlockSpec((M, L), lambda kb, jb: (0, 0))],
        out_specs=pl.BlockSpec((N, S, T, N), lambda kb, jb: (0, jb, kb, 0)),
        scratch_shapes=[pltpu.VMEM((N * S, M * S), BF16)],
        compiler_params=pltpu.CompilerParams(vmem_limit_bytes=LIMIT),
        name="expand",
    )(v2, b1_t)


def solution(mesh):
    vol_spec = P("mx", "my", "mz", "rhs")
    core_spec = P("mx", "my", "mz")
    full_spec = P()

    def local_operator(x_blk, fac_a1, fac_a2, fac_a3, diag_blk, fac_b1, fac_b2, fac_b3):
        v2 = compress(x_blk, fac_a1, fac_a2, fac_a3, fac_b2.T, fac_b3.T, diag_blk)
        return expand(v2, fac_b1.T)

    return jax.shard_map(local_operator, mesh=mesh, in_specs=(vol_spec, full_spec, full_spec, full_spec, core_spec, full_spec, full_spec, full_spec), out_specs=vol_spec, check_vma=False)
```

time: 888 us -> 191 us (0.22)
  waiting for transfers between devices: 497 us -> 0 us
  Pallas kernels: 0 us -> 189 us
  local copies, waits for them, and re-layouts: 185 us -> 1.58 us
  matrix products: 171 us -> 0 us
  other arithmetic: 20.9 us -> 0 us
  between operations: 13.5 us -> 0.01 us
    reduce_scatter x3 -> x0, waiting for transfers between devices: 316 us -> none  [the longest x1 188 us: local_operator(): lax.psum_scatter(part_two, 'my', scatter_dimension=1, tiled=True)]
    pallas_call x0 -> x2, Pallas kernels: none -> 189 us  [the longest x1 140 us: compress(): pl.pallas_call(compress_body, out_shape=jax.ShapeDtypeStruct((QUART, N, M...]
    all_gather x3 -> x0, waiting for transfers between devices: 181 us -> none  [the longest x1 102 us: local_operator(): v3_gathered = lax.all_gather(v_three, 'my', axis=1, tiled=True)]
    dot_general x4 -> x0, local copies, waits for them, and re-layouts: 172 us -> none  [the longest x1 88.8 us: local_operator(): jnp.einsum('ia,ajkr->ijkr', b1_rows, v2_gathered, preferred_element_type=...]
    dot_general x6 -> x0, matrix products: 171 us -> none  [the longest x1 69 us: local_operator(): jnp.einsum('ia,ajkr->ijkr', a1_cols, x_blk, preferred_element_type=jnp.fl...]
    convert_element_type x2 -> x0, other arithmetic: 20.9 us -> none  [the longest x1 18.2 us: local_operator(): lax.psum_scatter(part_one, 'mx', scatter_dimension=0, tiled=True)]
    all_gather x1 -> x0, local copies, waits for them, and re-layouts: 13.1 us -> none  [local_operator(): v3_gathered = lax.all_gather(v_three, 'my', axis=1, tiled=True)]
  transfers between devices with their start and end apart: 6 -> 0, of which waited for: 6 -> 0; matrix products, arithmetic and copies ran while one was open for 0% -> 0% of each run, Pallas kernels for 0% -> 0%
where the time goes in v1:
time: 191 us; the launch traced here: 190 us
  Pallas kernels  189 us (99%)
    pallas_call x1, Pallas kernels, compress(): pl.pallas_call(compress_body, out_shape=jax.ShapeDtypeStruct((QUART, N, M...  140 us
    pallas_call x1, Pallas kernels, expand(): pl.pallas_call(expand_body, grid=(QUART, N // S), out_shape=jax.ShapeDtyp...  48.8 us

profile of v1, /device:TPU:0, one launch (start us, length us, event | category | flops | bytes accessed | tf_op | source)
XLA Modules:
  0.0 190.2 jit_solution(12722390764945802753)
XLA Ops:
  0.0 1.6 copy.10.d_ref
  1.6 139.8 %compress.1.v2_ref = bf16[4,64,256,128]{3,2,1,0:T(8,128)(2,1)} custom-call(bf16[64,64,64,64]{3,2,1,0:T(8,128)(2,1)} %x_hbm.1, bf16[32,128]{1,0:T(8,128)(2,1)} %a1_ref.1, bf16[32,128]{1,0:T(8,128)(2,1)} %a2_ref.1, bf16[32,128]{1,0:T(8,128)(2,1)} %a3_ref.1, bf16[32,128]{1,0:T(8,128)(2,1)} %bitcast.7, bf16[32,128]{1,0:T(8,128)(2,1)} %bitcast.8, ...), custom_call_target="tpu_custom_call" | custom-call | tf_op jit(solution)/shard_map/compress/pallas_call | solution.py:385
  141.4 48.8 %expand.1 = f32[64,64,64,64]{3,2,1,0:T(8,128)} custom-call(bf16[4,64,256,128]{3,2,1,0:T(8,128)(2,1)} %compress.1.v2_ref, bf16[32,128]{1,0:T(8,128)(2,1)} %bitcast.9), custom_call_target="tpu_custom_call" | custom-call | tf_op jit(solution)/shard_map/expand/pallas_call | solution.py:422

commit v2 on v1

--- a/solution.py
+++ b/solution.py
@@ -20,11 +20,12 @@
 AHEAD = 4
 NEAR = 4
 STEPS = N // TWO
-EARLY = 10
-A, B, C, D, E = range(5)
-SIZES = (4, 6, 3, 2, 1)
-STARTS = (0, 4, 10, 13, 15)
-CHUNKS = (0, 0, 4, 2, 1)
+EARLY = 8
+A, B, C, D, E, G = range(6)
+SIZES = (4, 4, 4, 2, 1, 1)
+STARTS = (0, 4, 8, 12, 14, 15)
+CHUNKS = (0, 0, 4, 2, 1, 1)
+FILLER = 8
 GROUPS = range(len(SIZES))
 OTHERS = range(1, QUART)
 DEVICES = range(1, S)
@@ -84,12 +85,11 @@
     def send(src, dst, s_sem, r_sem, dev):
         return pltpu.make_async_remote_copy(src, dst, s_sem, r_sem, device_id=ids(dev), device_id_type=MESH)
 
-    peer, in_x, in_y = (oc, y, z), (c, oy, z), (c, y, oz)
+    peer, in_x, in_y, diagonal = (oc, y, z), (c, oy, z), (c, y, oz), (c, oy, oz)
 
     barrier = pltpu.get_barrier_semaphore()
     for rel in DEVICES:
         pl.semaphore_signal(barrier, inc=1, device_id=ids(flip(rel)), device_id_type=MESH)
-    pl.semaphore_wait(barrier, len(DEVICES))
 
     def half_of(core, t):
         return x_hbm.at[:, pl.ds(TWO * t, TWO), pl.ds(core * M, M), :]
@@ -102,28 +102,30 @@
         slot = lax.rem(t, RING)
         return send(half_of(oc, t), xr.at[slot], xs_sem.at[slot], xr_sem.at[slot], peer)
 
+    for t in range(NEAR - 1):
+        near(t).start()
+
+    def slot_of(dev):
+        return QUART * dev[0] + TWO * dev[1] + dev[2]
+
+    dall[slot_of((c, y, z))] = d_ref[...].reshape(H * H, H).T
+
+    def rows_one(p):
+        return lax.rem(p // T + H * y, M)
+
+    fill(k1o, a1_ref[...], rows_one, lambda q: c * N + q // T, alike(T))
+    fill(k1r, a1_ref[...], rows_one, lambda q: oc * N + q // T, alike(T))
+    pl.semaphore_wait(barrier, len(DEVICES))
     for t in range(AHEAD):
         cross(t).start()
-    for t in range(NEAR - 1):
-        near(t).start()
-
-    def slot_of(dev):
-        return QUART * dev[0] + TWO * dev[1] + dev[2]
 
     my_slot = slot_of((c, y, z))
 
     def diag(rel):
-        return send(d_ref, dall.at[my_slot], ds_sem.at[rel - 1], dr_sem.at[rel - 1], flip(rel))
+        return send(dall.at[my_slot], dall.at[my_slot], ds_sem.at[rel - 1], dr_sem.at[rel - 1], flip(rel))
 
     for rel in DEVICES:
         diag(rel).start()
-    dall[my_slot] = d_ref[...]
-
-    def rows_one(p):
-        return lax.rem(p // T + H * y, M)
-
-    fill(k1o, a1_ref[...], rows_one, lambda q: c * N + q // T, alike(T))
-    fill(k1r, a1_ref[...], rows_one, lambda q: oc * N + q // T, alike(T))
 
     def pack(ref, slot):
         parts = [jnp.concatenate([ref[slot, :, s, 0:T, :], ref[slot, :, s, T:M, :]], axis=-1).reshape(N * T, L)
@@ -148,6 +150,10 @@
         @pl.when(t >= 1)
         def _():
             early(t - 1).start()
+
+        @pl.when(t == 2 * FILLER + 1)
+        def _():
+            late(C, 0).start()
 
         near(t).wait()
         cross(t).wait_recv()
@@ -173,12 +179,12 @@
         def _():
             cross(t + AHEAD).start()
 
-    def depart(g):
-        for n in range(CHUNKS[g]):
+    def depart(g, first=0):
+        for n in range(first, CHUNKS[g]):
             late(g, n).start()
 
     early(STEPS - 1).start()
-    depart(C)
+    depart(C, 1)
     for t in range(STEPS - RING + AHEAD, STEPS):
         cross(t).wait_send()
 
@@ -257,18 +263,22 @@
         return send(wbuf.at[at], wbuf.at[at], ws_sem.at[g, kind], wr_sem.at[g, kind], dev)
 
     OWN_X, OWN_Y, OWN_P, X_Y, X_P, Y_P, D_P = range(KINDS)
-    diagonal = (c, oy, oz)
 
     def gather_first(g):
         for kind, dev in ((OWN_X, in_x), (OWN_Y, in_y), (OWN_P, peer)):
             share(g, kind, (c, y, z), dev).start()
-
-    def gather_rest(g):
+        if g == G:
+            share(g, X_Y, (c, y, z), diagonal).start()
+
+    def forward(g):
         share(g, OWN_X, in_x, in_x).wait_recv()
-        share(g, X_Y, in_x, in_y).start()
+        if g != G:
+            share(g, X_Y, in_x, in_y).start()
         share(g, X_P, in_x, peer).start()
         share(g, OWN_Y, in_y, in_y).wait_recv()
         share(g, Y_P, in_y, peer).start()
+
+    def forward_diagonal(g):
         share(g, X_Y, diagonal, in_y).wait_recv()
         share(g, D_P, diagonal, peer).start()
 
@@ -306,8 +316,8 @@
             v2s[slot, kb] = pair.astype(BF16)
         out_copy(p).start()
 
-    def all_middle(g):
-        @pl.loop(STARTS[g], STARTS[g] + SIZES[g])
+    def all_middle(g, first=0, count=None):
+        @pl.loop(STARTS[g] + first, STARTS[g] + (first + count if count else SIZES[g]))
         def _(p):
             middle(p)
 
@@ -325,37 +335,52 @@
     all_second(B)
     third(A)
     gather_first(A)
-    depart(D)
     third(B)
     gather_first(B)
+    depart(D)
+    depart(E)
     arrived(C)
     all_second(C)
-    gather_rest(A)
+    forward(A)
+    forward(B)
     third(C)
     gather_first(C)
-    depart(E)
+    depart(G)
+    forward_diagonal(A)
     gather_end(A)
     all_middle(A)
+    forward_diagonal(B)
     arrived(D)
     all_second(D)
-    gather_rest(B)
+    gather_end(B)
+    all_middle(B)
     third(D)
     gather_first(D)
-    gather_rest(C)
-    gather_end(B)
-    all_middle(B)
     arrived(E)
     all_second(E)
-    gather_end(C)
-    all_middle(C)
+    forward(C)
     third(E)
     gather_first(E)
-    gather_rest(D)
+    forward_diagonal(C)
+    arrived(G)
+    all_second(G)
+    forward(D)
+    gather_end(C)
+    all_middle(C, 0, TWO)
+    forward(E)
+    third(G)
+    gather_first(G)
+    all_middle(C, TWO)
+    forward_diagonal(D)
     gather_end(D)
+    forward(G)
     all_middle(D)
-    gather_rest(E)
+    forward_diagonal(E)
     gather_end(E)
     all_middle(E)
+    forward_diagonal(G)
+    gather_end(G)
+    all_middle(G)
 
     @pl.loop(0, STEPS)
     def _(t):
@@ -378,7 +403,6 @@
     vmem = pl.BlockSpec(memory_space=pltpu.VMEM)
     hbm = pl.BlockSpec(memory_space=pl.ANY)
     dma = pltpu.SemaphoreType.DMA
-    d_flat = d.transpose(2, 0, 1).reshape(H, H * H)
     u1 = pltpu.VMEM((N, H * T, L), BF16)
     spread = pltpu.VMEM((M * T, N * T), BF16)
     groups = len(SIZES)
@@ -401,7 +425,7 @@
         ],
         compiler_params=pltpu.CompilerParams(collective_id=0, has_side_effects=True, vmem_limit_bytes=LIMIT),
         name="compress",
-    )(x, a1, a2, a3, b2_t, b3_t, d_flat)
+    )(x, a1, a2, a3, b2_t, b3_t, d)
 
 
 def expand_body(v2_ref, b1_ref, z_ref, l1):

time: 191 us -> 176 us (0.921)
  Pallas kernels: 189 us -> 176 us
    pallas_call x1, Pallas kernels: 140 us -> 127 us  [compress(): pl.pallas_call(compress_body, out_shape=jax.ShapeDtypeStruct((QUART, N, M...]
where the time goes in v2:
time: 176 us
  Pallas kernels  176 us (100%)
    pallas_call x1, Pallas kernels, compress(): pl.pallas_call(compress_body, out_shape=jax.ShapeDtypeStruct((QUART, N, M...  127 us
    pallas_call x1, Pallas kernels, expand(): pl.pallas_call(expand_body, grid=(QUART, N // S), out_shape=jax.ShapeDtyp...  48.8 us

profile of v2, /device:TPU:0, one launch (start us, length us, event | category | flops | bytes accessed | tf_op | source)
XLA Modules:
  0.0 175.6 jit_solution(2884034430835657862)
XLA Ops:
  0.0 126.8 %compress.1.v2_ref = bf16[4,64,256,128]{3,2,1,0:T(8,128)(2,1)} custom-call(bf16[64,64,64,64]{3,2,1,0:T(8,128)(2,1)} %x_hbm.1, bf16[32,128]{1,0:T(8,128)(2,1)} %a1_ref.1, bf16[32,128]{1,0:T(8,128)(2,1)} %a2_ref.1, bf16[32,128]{1,0:T(8,128)(2,1)} %a3_ref.1, bf16[32,128]{1,0:T(8,128)(2,1)} %bitcast.3, bf16[32,128]{1,0:T(8,128)(2,1)} %bitcast.4, f32[16,16,16]{2,1,0:T(8,128)} %d_ref.1), custom_call_target="tpu_custom_call" | custom-call | tf_op jit(solution)/shard_map/compress/pallas_call | solution.py:409
  126.8 48.8 %expand.1 = f32[64,64,64,64]{3,2,1,0:T(8,128)} custom-call(bf16[4,64,256,128]{3,2,1,0:T(8,128)(2,1)} %compress.1.v2_ref, bf16[32,128]{1,0:T(8,128)(2,1)} %bitcast.5), custom_call_target="tpu_custom_call" | custom-call | tf_op jit(solution)/shard_map/expand/pallas_call | solution.py:446

commit v3 on v2

--- a/solution.py
+++ b/solution.py
@@ -30,7 +30,8 @@
 OTHERS = range(1, QUART)
 DEVICES = range(1, S)
 KINDS = 7
-LIMIT = 62 * 1024 * 1024
+COLUMNS = 16
+LIMIT = 42 * 1024 * 1024
 
 
 def dot(a, b):
@@ -64,10 +65,10 @@
     return lambda p, q: lax.rem(p, n) == lax.rem(q, n)
 
 
-def compress_body(x_hbm, a1_ref, a2_ref, a3_ref, b2_ref, b3_ref, d_ref, v2_out,
-                  xl, xr, u1o, u1s, u1r, k1o, k1r, k2o, k2r, k3, l3, l2, u2s, u2b, wbuf, dall, v3, v2s,
-                  near_sem, xs_sem, xr_sem, credit, us_sem, ur_sem, gs_sem, gr_sem,
-                  vs_sem, vr_sem, ws_sem, wr_sem, ds_sem, dr_sem, out_sem):
+def compress_body(x_hbm, a1_ref, a2_ref, a3_ref, b1_ref, b2_ref, b3_ref, d_ref, v2_out, l1_out,
+                  xl, xr, u1o, u1s, u1r, k1o, k1r, k2o, k2r, k3, l3, l2, u2s, u2b, wbuf, dall, v3,
+                  near_sem, xs_sem, xr_sem, credit, u1_sem, late_s, late_r,
+                  u2_s, u2_r, w_s, w_r, d_sem):
     c = lax.axis_index("mx")
     y = lax.axis_index("my")
     z = lax.axis_index("mz")
@@ -122,7 +123,7 @@
     my_slot = slot_of((c, y, z))
 
     def diag(rel):
-        return send(dall.at[my_slot], dall.at[my_slot], ds_sem.at[rel - 1], dr_sem.at[rel - 1], flip(rel))
+        return send(dall.at[my_slot], dall.at[my_slot], d_sem.at[0], d_sem.at[1], flip(rel))
 
     for rel in DEVICES:
         diag(rel).start()
@@ -134,12 +135,12 @@
 
     def early(t):
         part = (pl.ds(TWO * t, TWO), pl.ds(0, EARLY * T))
-        return send(u1s.at[part], u1r.at[part], us_sem.at[t], ur_sem.at[t], in_x)
+        return send(u1s.at[part], u1r.at[part], u1_sem.at[0], u1_sem.at[1], in_x)
 
     def late(g, n):
         span = N // CHUNKS[g]
         part = (pl.ds(span * n, span), pl.ds(STARTS[g] * T, SIZES[g] * T))
-        return send(u1s.at[part], u1r.at[part], gs_sem.at[g, n], gr_sem.at[g, n], in_x)
+        return send(u1s.at[part], u1r.at[part], late_s, late_r.at[g], in_x)
 
     @pl.loop(0, STEPS)
     def _(t):
@@ -196,6 +197,7 @@
         sel = ones_where(iota((L, N), 0) == k_first + T * half)
         k3[half * M:(half + 1) * M, :] = dot(a3_ref[...], sel).astype(BF16)
     fill(l2, b2_ref[...], lambda p: y * N + p // S, lambda q: q // S, alike(S), dot_t)
+    fill(l1_out, b1_ref[...], lambda p: c * N + p // S, lambda q: lax.rem(q // S, TWO) * H + q // T, alike(S), dot_t)
     fill(l3, b3_ref[...], lambda p: z * N + p // L * T + lax.rem(p, T), lambda q: lax.rem(q, M),
          lambda p, q: lax.rem(p, L) // T == q // M, dot_t)
 
@@ -217,7 +219,7 @@
         dev = beside(rel)
         i_span = pl.ds(STARTS[g], SIZES[g])
         return send(u2s.at[i_span, pl.ds(quarter(dev) * L, L)], u2b.at[rel - 1, i_span],
-                    vs_sem.at[g, rel], vr_sem.at[g, rel], dev)
+                    u2_s, u2_r.at[g], dev)
 
     def all_second(g):
         if SIZES[g] >= TWO:
@@ -233,8 +235,8 @@
     lane = iota((M, TWO * L), 1)
 
     def third(g):
-        for rel in OTHERS:
-            inner(g, rel).wait_recv()
+        got = u2b.at[:, pl.ds(STARTS[g], SIZES[g])]
+        send(got, got, u2_s, u2_r.at[g], peer).wait_recv()
         base = slot_of((y, c, 0))
         d = jnp.concatenate([dall[base], dall[base + 1]], axis=0)
 
@@ -260,9 +262,10 @@
 
     def share(g, kind, owner, dev):
         at = (pl.ds(owner[1] * H + STARTS[g], SIZES[g]), pl.ds(quarter(owner) * QUART, QUART))
-        return send(wbuf.at[at], wbuf.at[at], ws_sem.at[g, kind], wr_sem.at[g, kind], dev)
-
-    OWN_X, OWN_Y, OWN_P, X_Y, X_P, Y_P, D_P = range(KINDS)
+        return send(wbuf.at[at], wbuf.at[at], w_s, w_r.at[g, min(kind, FROM_P)], dev)
+
+    OWN_X, OWN_Y, X_Y, OWN_P, X_P, Y_P, D_P = range(KINDS)
+    FROM_P = OWN_P
 
     def gather_first(g):
         for kind, dev in ((OWN_X, in_x), (OWN_Y, in_y), (OWN_P, peer)):
@@ -283,22 +286,12 @@
         share(g, D_P, diagonal, peer).start()
 
     def gather_end(g):
-        for kind, owner in ((OWN_P, (c, y, z)), (X_P, in_x), (Y_P, in_y), (D_P, diagonal)):
-            share(g, kind, (oc,) + owner[1:], peer).wait_recv()
+        got = wbuf.at[pl.ds(0, SIZES[g]), :]
+        send(got, got, w_s, w_r.at[g, FROM_P], peer).wait_recv()
 
     low_v = iota((QUART, S, S, L), TWO + 1) < N
 
-    def out_copy(p):
-        slot = lax.rem(p, TWO)
-        return pltpu.make_async_copy(
-            v2s.at[slot], v2_out.at[:, :, pl.ds(pl.multiple_of(p * T, T), T), :], out_sem.at[slot])
-
     def middle(p):
-        @pl.when(p >= TWO)
-        def _():
-            out_copy(p - TWO).wait()
-
-        slot = lax.rem(p, TWO)
         for jo in range(TWO):
             rhs = jnp.concatenate(
                 [wbuf[p + H * s, jo * S:(jo + 1) * S].reshape(TWO * L, L) for s in range(TWO)], axis=1)
@@ -313,24 +306,22 @@
         for kb in range(QUART):
             out = dot(l2[...], jnp.concatenate([v3[kb, 0], v3[kb, 1]], axis=1))
             pair = jnp.concatenate([out[:, :L].reshape(N, S, L), out[:, L:].reshape(N, S, L)], axis=1)
-            v2s[slot, kb] = pair.astype(BF16)
-        out_copy(p).start()
-
-    def all_middle(g, first=0, count=None):
-        @pl.loop(STARTS[g] + first, STARTS[g] + (first + count if count else SIZES[g]))
+            v2_out[kb, :, pl.ds(pl.multiple_of(p * T, T), T), :] = pair.astype(BF16)
+
+    def all_middle(g):
+        @pl.loop(STARTS[g], STARTS[g] + SIZES[g])
         def _(p):
             middle(p)
 
     def arrived(g):
-        for n in range(CHUNKS[g]):
-            late(g, n).wait_recv()
-
-    @pl.loop(0, STEPS)
-    def _(t):
-        early(t).wait_recv()
-
-    for rel in DEVICES:
-        diag(rel).wait_recv()
+        got = u1r.at[:, pl.ds(STARTS[g] * T, SIZES[g] * T)]
+        send(got, got, late_s, late_r.at[g], in_x).wait_recv()
+
+    first = u1r.at[:, pl.ds(0, EARLY * T)]
+    rest = u1r.at[:, pl.ds(EARLY * T, EARLY * T)]
+    cores = dall.at[pl.ds(0, len(DEVICES))]
+    send(first, first, u1_sem.at[0], u1_sem.at[1], in_x).wait_recv()
+    send(cores, cores, d_sem.at[0], d_sem.at[1], peer).wait_recv()
     all_second(A)
     all_second(B)
     third(A)
@@ -338,13 +329,13 @@
     third(B)
     gather_first(B)
     depart(D)
-    depart(E)
     arrived(C)
     all_second(C)
     forward(A)
     forward(B)
     third(C)
     gather_first(C)
+    depart(E)
     depart(G)
     forward_diagonal(A)
     gather_end(A)
@@ -352,54 +343,44 @@
     forward_diagonal(B)
     arrived(D)
     all_second(D)
+    forward(C)
     gather_end(B)
     all_middle(B)
     third(D)
     gather_first(D)
+    forward_diagonal(C)
     arrived(E)
     all_second(E)
-    forward(C)
+    gather_end(C)
+    all_middle(C)
     third(E)
     gather_first(E)
-    forward_diagonal(C)
     arrived(G)
     all_second(G)
     forward(D)
-    gather_end(C)
-    all_middle(C, 0, TWO)
     forward(E)
     third(G)
     gather_first(G)
-    all_middle(C, TWO)
     forward_diagonal(D)
     gather_end(D)
-    forward(G)
     all_middle(D)
     forward_diagonal(E)
     gather_end(E)
+    forward(G)
     all_middle(E)
     forward_diagonal(G)
     gather_end(G)
     all_middle(G)
 
-    @pl.loop(0, STEPS)
-    def _(t):
-        early(t).wait_send()
-
-    for rel in DEVICES:
-        diag(rel).wait_send()
-    for g in GROUPS:
-        for n in range(CHUNKS[g]):
-            late(g, n).wait_send()
-        for rel in OTHERS:
-            inner(g, rel).wait_send()
-        for kind in range(KINDS):
-            share(g, kind, (c, y, z), peer).wait_send()
-    out_copy(H - TWO).wait()
-    out_copy(H - 1).wait()
-
-
-def compress(x, a1, a2, a3, b2_t, b3_t, d):
+    sent = wbuf.at[pl.ds(0, KINDS * QUART), :]
+    send(first, first, u1_sem.at[0], u1_sem.at[1], in_x).wait_send()
+    send(rest, rest, late_s, late_r.at[0], in_x).wait_send()
+    send(cores, cores, d_sem.at[0], d_sem.at[1], peer).wait_send()
+    send(u2b, u2b, u2_s, u2_r.at[0], peer).wait_send()
+    send(sent, sent, w_s, w_r.at[0, 0], peer).wait_send()
+
+
+def compress(x, a1, a2, a3, b1_t, b2_t, b3_t, d):
     vmem = pl.BlockSpec(memory_space=pltpu.VMEM)
     hbm = pl.BlockSpec(memory_space=pl.ANY)
     dma = pltpu.SemaphoreType.DMA
@@ -408,52 +389,44 @@
     groups = len(SIZES)
     return pl.pallas_call(
         compress_body,
-        out_shape=jax.ShapeDtypeStruct((QUART, N, M * S, L), BF16),
-        in_specs=[hbm] + [vmem] * 6,
-        out_specs=hbm,
+        out_shape=(pltpu.VMEM((QUART, N, M * S, L), BF16), pltpu.VMEM((N * S, M * S), BF16)),
+        in_specs=[hbm] + [vmem] * 7,
+        out_specs=(vmem, vmem),
         scratch_shapes=[
             pltpu.VMEM((NEAR, N, TWO, M, N), BF16), pltpu.VMEM((RING, N, TWO, M, N), BF16), u1, u1, u1,
             spread, spread, spread, spread, pltpu.VMEM((N, N), BF16),
             pltpu.VMEM((M * T, M * S), BF16), pltpu.VMEM((N * S, M * S), BF16),
             pltpu.VMEM((H, M * T, L), BF16), pltpu.VMEM((len(OTHERS), H, L, L), BF16),
             pltpu.VMEM((M, H, M, L), BF16), pltpu.VMEM((S, H, H * H), F32),
-            pltpu.VMEM((QUART, TWO, M * S, L), BF16), pltpu.VMEM((TWO, QUART, N, T, L), BF16),
+            pltpu.VMEM((QUART, TWO, M * S, L), BF16),
             dma((NEAR,)), dma((RING,)), dma((RING,)), pltpu.SemaphoreType.REGULAR,
-            dma((STEPS,)), dma((STEPS,)), dma((groups, QUART)), dma((groups, QUART)),
-            dma((groups, QUART)), dma((groups, QUART)), dma((groups, KINDS)), dma((groups, KINDS)),
-            dma((KINDS,)), dma((KINDS,)), dma((TWO,)),
+            dma((TWO,)), dma, dma((groups,)), dma, dma((groups,)), dma, dma((groups, QUART)), dma((TWO,)),
         ],
         compiler_params=pltpu.CompilerParams(collective_id=0, has_side_effects=True, vmem_limit_bytes=LIMIT),
         name="compress",
-    )(x, a1, a2, a3, b2_t, b3_t, d)
-
-
-def expand_body(v2_ref, b1_ref, z_ref, l1):
-    @pl.when((pl.program_id(0) == 0) & (pl.program_id(1) == 0))
-    def _():
-        c = lax.axis_index("mx")
-        fill(l1, b1_ref[...], lambda p: c * N + p // S, lambda q: lax.rem(q // S, TWO) * H + q // T, alike(S), dot_t)
-
-    for j in range(0, z_ref.shape[1], TWO):
-        out = dot(l1[...], jnp.concatenate([v2_ref[0, j], v2_ref[0, j + 1]], axis=1))
+    )(x, a1, a2, a3, b1_t, b2_t, b3_t, d)
+
+
+def expand_body(v2_ref, l1_ref, z_ref):
+    for j in range(0, COLUMNS, TWO):
+        out = dot(l1_ref[...], jnp.concatenate([v2_ref[0, j], v2_ref[0, j + 1]], axis=1))
         for s in range(TWO):
             o = out[:, s * L:(s + 1) * L].reshape(N, S, L)
             z_ref[:, j + s, :S, :] = o[:, :, :N]
             z_ref[:, j + s, S:, :] = pltpu.roll(o, N, TWO)[:, :, :N]
 
 
-def expand(v2, b1_t):
+def expand(v2, l1):
     return pl.pallas_call(
         expand_body,
-        grid=(QUART, N // S),
+        grid=(QUART, N // COLUMNS),
         out_shape=jax.ShapeDtypeStruct((N, N, N, N), F32),
-        in_specs=[pl.BlockSpec((1, S, M * S, L), lambda kb, jb: (kb, jb, 0, 0)),
-                  pl.BlockSpec((M, L), lambda kb, jb: (0, 0))],
-        out_specs=pl.BlockSpec((N, S, T, N), lambda kb, jb: (0, jb, kb, 0)),
-        scratch_shapes=[pltpu.VMEM((N * S, M * S), BF16)],
-        compiler_params=pltpu.CompilerParams(vmem_limit_bytes=LIMIT),
+        in_specs=[pl.BlockSpec((1, COLUMNS, M * S, L), lambda kb, jb: (kb, jb, 0, 0)),
+                  pl.BlockSpec((N * S, M * S), lambda kb, jb: (0, 0))],
+        out_specs=pl.BlockSpec((N, COLUMNS, T, N), lambda kb, jb: (0, jb, kb, 0)),
+        compiler_params=pltpu.CompilerParams(vmem_limit_bytes=LIMIT // 2),
         name="expand",
-    )(v2, b1_t)
+    )(v2, l1)
 
 
 def solution(mesh):
@@ -462,7 +435,7 @@
     full_spec = P()
 
     def local_operator(x_blk, fac_a1, fac_a2, fac_a3, diag_blk, fac_b1, fac_b2, fac_b3):
-        v2 = compress(x_blk, fac_a1, fac_a2, fac_a3, fac_b2.T, fac_b3.T, diag_blk)
-        return expand(v2, fac_b1.T)
+        v2, l1 = compress(x_blk, fac_a1, fac_a2, fac_a3, fac_b1.T, fac_b2.T, fac_b3.T, diag_blk)
+        return expand(v2, l1)
 
     return jax.shard_map(local_operator, mesh=mesh, in_specs=(vol_spec, full_spec, full_spec, full_spec, core_spec, full_spec, full_spec, full_spec), out_specs=vol_spec, check_vma=False)

time: 176 us -> 165 us (0.938)
  Pallas kernels: 176 us -> 165 us
    pallas_call x2, Pallas kernels: 176 us -> 165 us  [the longest x1 122 us: compress(): pl.pallas_call(compress_body, out_shape=(pltpu.VMEM((QUART, N, M * S, L),...]
where the time goes in v3:
time: 165 us
  Pallas kernels  165 us (100%)
    pallas_call x1, Pallas kernels, compress(): pl.pallas_call(compress_body, out_shape=(pltpu.VMEM((QUART, N, M * S, L),...  122 us
    pallas_call x1, Pallas kernels, expand(): pl.pallas_call(expand_body, grid=(QUART, N // COLUMNS), out_shape=jax.Sha...  42.8 us

profile of v3, /device:TPU:0, one launch (start us, length us, event | category | flops | bytes accessed | tf_op | source)
XLA Modules:
  0.0 164.6 jit_solution(12504181379308959866)
XLA Ops:
  0.0 121.7 %compress.1 = (bf16[4,64,256,128]{3,2,1,0:T(8,128)(2,1)S(1)}, bf16[512,256]{1,0:T(8,128)(2,1)S(1)}) custom-call(bf16[64,64,64,64]{3,2,1,0:T(8,128)(2,1)} %x_hbm.1, bf16[32,128]{1,0:T(8,128)(2,1)} %a1_ref.1, bf16[32,128]{1,0:T(8,128)(2,1)} %a2_ref.1, bf16[32,128]{1,0:T(8,128)(2,1)} %a3_ref.1, bf16[32,128]{1,0:T(8,128)(2,1)} %bitcast.3, ...), custom_call_target="tpu_custom_call" | custom-call | tf_op jit(solution)/shard_map/compress/pallas_call | solution.py:390
  121.7 42.8 %expand.1 = f32[64,64,64,64]{3,2,1,0:T(8,128)} custom-call(bf16[4,64,256,128]{3,2,1,0:T(8,128)(2,1)S(1)} %get-tuple-element.7.v2_ref, bf16[512,256]{1,0:T(8,128)(2,1)S(1)} %get-tuple-element.8.l1_ref), custom_call_target="tpu_custom_call" | custom-call | tf_op jit(solution)/shard_map/expand/pallas_call | solution.py:420

commit v4 on v3

--- a/solution.py
+++ b/solution.py
@@ -30,7 +30,8 @@
 OTHERS = range(1, QUART)
 DEVICES = range(1, S)
 KINDS = 7
-COLUMNS = 16
+COLUMNS = 4
+SLOTS = 4
 LIMIT = 42 * 1024 * 1024
 
 
@@ -103,22 +104,22 @@
         slot = lax.rem(t, RING)
         return send(half_of(oc, t), xr.at[slot], xs_sem.at[slot], xr_sem.at[slot], peer)
 
-    for t in range(NEAR - 1):
-        near(t).start()
-
-    def slot_of(dev):
-        return QUART * dev[0] + TWO * dev[1] + dev[2]
-
-    dall[slot_of((c, y, z))] = d_ref[...].reshape(H * H, H).T
-
-    def rows_one(p):
-        return lax.rem(p // T + H * y, M)
-
-    fill(k1o, a1_ref[...], rows_one, lambda q: c * N + q // T, alike(T))
-    fill(k1r, a1_ref[...], rows_one, lambda q: oc * N + q // T, alike(T))
     pl.semaphore_wait(barrier, len(DEVICES))
     for t in range(AHEAD):
         cross(t).start()
+    for t in range(NEAR - 1):
+        near(t).start()
+
+    def slot_of(dev):
+        return QUART * dev[0] + TWO * dev[1] + dev[2]
+
+    dall[slot_of((c, y, z))] = d_ref[...].reshape(H * H, H).T
+
+    def rows_one(p):
+        return lax.rem(p // T + H * y, M)
+
+    fill(k1o, a1_ref[...], rows_one, lambda q: c * N + q // T, alike(T))
+    fill(k1r, a1_ref[...], rows_one, lambda q: oc * N + q // T, alike(T))
 
     my_slot = slot_of((c, y, z))
 
@@ -152,7 +153,7 @@
         def _():
             early(t - 1).start()
 
-        @pl.when(t == 2 * FILLER + 1)
+        @pl.when(t == FILLER + 1)
         def _():
             late(C, 0).start()
 
@@ -362,13 +363,13 @@
     third(G)
     gather_first(G)
     forward_diagonal(D)
+    forward_diagonal(E)
     gather_end(D)
     all_middle(D)
-    forward_diagonal(E)
+    forward(G)
+    forward_diagonal(G)
     gather_end(E)
-    forward(G)
     all_middle(E)
-    forward_diagonal(G)
     gather_end(G)
     all_middle(G)
 
@@ -407,23 +408,43 @@
     )(x, a1, a2, a3, b1_t, b2_t, b3_t, d)
 
 
-def expand_body(v2_ref, l1_ref, z_ref):
-    for j in range(0, COLUMNS, TWO):
-        out = dot(l1_ref[...], jnp.concatenate([v2_ref[0, j], v2_ref[0, j + 1]], axis=1))
-        for s in range(TWO):
-            o = out[:, s * L:(s + 1) * L].reshape(N, S, L)
-            z_ref[:, j + s, :S, :] = o[:, :, :N]
-            z_ref[:, j + s, S:, :] = pltpu.roll(o, N, TWO)[:, :, :N]
+def expand_body(v2_ref, l1_ref, z_hbm, zbuf, z_sem):
+    per_block = N // COLUMNS
+
+    def leave(n):
+        slot = lax.rem(n, SLOTS)
+        where = (slice(None), pl.ds(n % per_block * COLUMNS, COLUMNS), pl.ds(n // per_block * T, T))
+        return pltpu.make_async_copy(zbuf.at[slot], z_hbm.at[where], z_sem.at[slot])
+
+    @pl.loop(0, QUART * per_block)
+    def _(n):
+        slot = lax.rem(n, SLOTS)
+
+        @pl.when(n >= SLOTS)
+        def _():
+            leave(n - SLOTS).wait()
+
+        for j in range(0, COLUMNS, TWO):
+            at = n % per_block * COLUMNS + j
+            out = dot(l1_ref[...], jnp.concatenate([v2_ref[n // per_block, at + s] for s in range(TWO)], axis=1))
+            for s in range(TWO):
+                o = out[:, s * L:(s + 1) * L].reshape(N, S, L)
+                zbuf[slot, :, j + s, :S, :] = o[:, :, :N]
+                zbuf[slot, :, j + s, S:, :] = pltpu.roll(o, N, TWO)[:, :, :N]
+        leave(n).start()
+
+    for n in range(QUART * per_block - SLOTS, QUART * per_block):
+        leave(n).wait()
 
 
 def expand(v2, l1):
+    vmem = pl.BlockSpec(memory_space=pltpu.VMEM)
     return pl.pallas_call(
         expand_body,
-        grid=(QUART, N // COLUMNS),
         out_shape=jax.ShapeDtypeStruct((N, N, N, N), F32),
-        in_specs=[pl.BlockSpec((1, COLUMNS, M * S, L), lambda kb, jb: (kb, jb, 0, 0)),
-                  pl.BlockSpec((N * S, M * S), lambda kb, jb: (0, 0))],
-        out_specs=pl.BlockSpec((N, COLUMNS, T, N), lambda kb, jb: (0, jb, kb, 0)),
+        in_specs=[vmem, vmem],
+        out_specs=pl.BlockSpec(memory_space=pl.ANY),
+        scratch_shapes=[pltpu.VMEM((SLOTS, N, COLUMNS, T, N), F32), pltpu.SemaphoreType.DMA((SLOTS,))],
         compiler_params=pltpu.CompilerParams(vmem_limit_bytes=LIMIT // 2),
         name="expand",
     )(v2, l1)

time: 165 us -> 162 us (0.982)
  Pallas kernels: 165 us -> 162 us
where the time goes in v4:
time: 162 us
  Pallas kernels  162 us (100%)
    pallas_call x1, Pallas kernels, compress(): pl.pallas_call(compress_body, out_shape=(pltpu.VMEM((QUART, N, M * S, L),...  121 us
    pallas_call x1, Pallas kernels, expand(): pl.pallas_call(expand_body, out_shape=jax.ShapeDtypeStruct((N, N, N, N),...  41.7 us

profile of v4, /device:TPU:0, one launch (start us, length us, event | category | flops | bytes accessed | tf_op | source)
XLA Modules:
  0.0 162.3 jit_solution(14491264527542666294)
XLA Ops:
  0.0 120.6 %compress.1 = (bf16[4,64,256,128]{3,2,1,0:T(8,128)(2,1)S(1)}, bf16[512,256]{1,0:T(8,128)(2,1)S(1)}) custom-call(bf16[64,64,64,64]{3,2,1,0:T(8,128)(2,1)} %x_hbm.1, bf16[32,128]{1,0:T(8,128)(2,1)} %a1_ref.1, bf16[32,128]{1,0:T(8,128)(2,1)} %a2_ref.1, bf16[32,128]{1,0:T(8,128)(2,1)} %a3_ref.1, bf16[32,128]{1,0:T(8,128)(2,1)} %bitcast.3, ...), custom_call_target="tpu_custom_call" | custom-call | tf_op jit(solution)/shard_map/compress/pallas_call | solution.py:391
  120.6 41.7 %expand.1 = f32[64,64,64,64]{3,2,1,0:T(8,128)} custom-call(bf16[4,64,256,128]{3,2,1,0:T(8,128)(2,1)S(1)} %get-tuple-element.7.v2_ref, bf16[512,256]{1,0:T(8,128)(2,1)S(1)} %get-tuple-element.8.l1_ref), custom_call_target="tpu_custom_call" | custom-call | tf_op jit(solution)/shard_map/expand/pallas_call | solution.py:442

commit v5 on v4

--- a/solution.py
+++ b/solution.py
@@ -21,11 +21,12 @@
 NEAR = 4
 STEPS = N // TWO
 EARLY = 8
-A, B, C, D, E, G = range(6)
-SIZES = (4, 4, 4, 2, 1, 1)
-STARTS = (0, 4, 8, 12, 14, 15)
-CHUNKS = (0, 0, 4, 2, 1, 1)
-FILLER = 8
+A, B, C, D, E, F, G = range(7)
+SIZES = (4, 4, 2, 2, 2, 1, 1)
+STARTS = (0, 4, 8, 10, 12, 14, 15)
+CHUNKS = (0, 0, 4, 2, 2, 1, 1)
+DIRECT = (F, G)
+FILLERS = 2
 GROUPS = range(len(SIZES))
 OTHERS = range(1, QUART)
 DEVICES = range(1, S)
@@ -66,10 +67,10 @@
     return lambda p, q: lax.rem(p, n) == lax.rem(q, n)
 
 
-def compress_body(x_hbm, a1_ref, a2_ref, a3_ref, b1_ref, b2_ref, b3_ref, d_ref, v2_out, l1_out,
-                  xl, xr, u1o, u1s, u1r, k1o, k1r, k2o, k2r, k3, l3, l2, u2s, u2b, wbuf, dall, v3,
+def compress_body(x_hbm, a1_hbm, a2_hbm, a3_hbm, b1_hbm, b2_hbm, b3_hbm, d_hbm, v2_out, l1_out,
+                  fac, d_ref, xl, xr, u1o, u1s, u1r, k1o, k1r, k2o, k2r, k3, l3, l2, u2s, u2b, wbuf, dall, v3,
                   near_sem, xs_sem, xr_sem, credit, u1_sem, late_s, late_r,
-                  u2_s, u2_r, w_s, w_r, d_sem):
+                  u2_s, u2_r, w_s, w_r, d_sem, in_sem):
     c = lax.axis_index("mx")
     y = lax.axis_index("my")
     z = lax.axis_index("mz")
@@ -104,12 +105,21 @@
         slot = lax.rem(t, RING)
         return send(half_of(oc, t), xr.at[slot], xs_sem.at[slot], xr_sem.at[slot], peer)
 
+    loads = [pltpu.make_async_copy(src, fac.at[n], in_sem.at[n])
+             for n, src in enumerate((a1_hbm, a2_hbm, a3_hbm, b1_hbm, b2_hbm, b3_hbm))]
+    loads.append(pltpu.make_async_copy(d_hbm, d_ref, in_sem.at[len(loads)]))
+    for load in loads:
+        load.start()
+    a1_ref, a2_ref, a3_ref, b1_ref, b2_ref, b3_ref = (fac.at[n] for n in range(len(loads) - 1))
     pl.semaphore_wait(barrier, len(DEVICES))
     for t in range(AHEAD):
         cross(t).start()
     for t in range(NEAR - 1):
         near(t).start()
 
+    for load in loads:
+        load.wait()
+
     def slot_of(dev):
         return QUART * dev[0] + TWO * dev[1] + dev[2]
 
@@ -153,9 +163,10 @@
         def _():
             early(t - 1).start()
 
-        @pl.when(t == FILLER + 1)
-        def _():
-            late(C, 0).start()
+        for n in range(FILLERS):
+            @pl.when(t == S * (n + 1) + 1)
+            def _(n=n):
+                late(C, n).start()
 
         near(t).wait()
         cross(t).wait_recv()
@@ -186,7 +197,8 @@
             late(g, n).start()
 
     early(STEPS - 1).start()
-    depart(C, 1)
+    depart(C, FILLERS)
+    depart(D)
     for t in range(STEPS - RING + AHEAD, STEPS):
         cross(t).wait_send()
 
@@ -198,7 +210,7 @@
         sel = ones_where(iota((L, N), 0) == k_first + T * half)
         k3[half * M:(half + 1) * M, :] = dot(a3_ref[...], sel).astype(BF16)
     fill(l2, b2_ref[...], lambda p: y * N + p // S, lambda q: q // S, alike(S), dot_t)
-    fill(l1_out, b1_ref[...], lambda p: c * N + p // S, lambda q: lax.rem(q // S, TWO) * H + q // T, alike(S), dot_t)
+    fill(l1_out, b1_ref[...], lambda p: c * N + p // S, lambda q: q // S, alike(S), dot_t)
     fill(l3, b3_ref[...], lambda p: z * N + p // L * T + lax.rem(p, T), lambda q: lax.rem(q, M),
          lambda p, q: lax.rem(p, L) // T == q // M, dot_t)
 
@@ -207,9 +219,12 @@
             return jnp.concatenate(
                 [ref[:, pl.ds(pl.multiple_of((i + s) * T, T), T), :].reshape(N * T, L) for s in range(width)], axis=1)
 
-        out = dot(k2o[...], side(u1o)) + dot(k2r[...], side(u1r))
-        for s in range(width):
-            u2s[i + s] = out[:, s * L:(s + 1) * L].astype(BF16)
+        own, got = side(u1o), side(u1r)
+        part = M * T * width // TWO
+        for r0 in range(0, M * T, part):
+            out = dot(k2o[r0:r0 + part, :], own) + dot(k2r[r0:r0 + part, :], got)
+            for s in range(width):
+                u2s[i + s, r0:r0 + part, :] = out[:, s * L:(s + 1) * L].astype(BF16)
 
     def quarter(dev):
         return TWO * dev[0] + dev[2]
@@ -263,39 +278,45 @@
 
     def share(g, kind, owner, dev):
         at = (pl.ds(owner[1] * H + STARTS[g], SIZES[g]), pl.ds(quarter(owner) * QUART, QUART))
-        return send(wbuf.at[at], wbuf.at[at], w_s, w_r.at[g, min(kind, FROM_P)], dev)
-
-    OWN_X, OWN_Y, X_Y, OWN_P, X_P, Y_P, D_P = range(KINDS)
-    FROM_P = OWN_P
-
-    def gather_first(g):
-        for kind, dev in ((OWN_X, in_x), (OWN_Y, in_y), (OWN_P, peer)):
-            share(g, kind, (c, y, z), dev).start()
-        if g == G:
+        return send(wbuf.at[at], wbuf.at[at], w_s, w_r.at[g, BY_KIND[kind]], dev)
+
+    OWN_X, OWN_Y, X_Y, OWN_P, Y_P, X_P, D_P = range(KINDS)
+    SAME, OTHER = OWN_P, OWN_P + 1
+    BY_KIND = (OWN_X, OWN_Y, X_Y, SAME, SAME, OTHER, OTHER)
+
+    def gather_near(g):
+        share(g, OWN_Y, (c, y, z), in_y).start()
+        share(g, OWN_P, (c, y, z), peer).start()
+
+    def gather_far(g):
+        share(g, OWN_X, (c, y, z), in_x).start()
+        if g in DIRECT:
             share(g, X_Y, (c, y, z), diagonal).start()
 
-    def forward(g):
+    def forward_near(g):
+        share(g, OWN_Y, in_y, in_y).wait_recv()
+        share(g, Y_P, in_y, peer).start()
+
+    def forward_far(g):
         share(g, OWN_X, in_x, in_x).wait_recv()
-        if g != G:
+        if g not in DIRECT:
             share(g, X_Y, in_x, in_y).start()
         share(g, X_P, in_x, peer).start()
-        share(g, OWN_Y, in_y, in_y).wait_recv()
-        share(g, Y_P, in_y, peer).start()
 
     def forward_diagonal(g):
         share(g, X_Y, diagonal, in_y).wait_recv()
         share(g, D_P, diagonal, peer).start()
 
-    def gather_end(g):
-        got = wbuf.at[pl.ds(0, SIZES[g]), :]
-        send(got, got, w_s, w_r.at[g, FROM_P], peer).wait_recv()
+    def gathered(g, side):
+        got = wbuf.at[pl.ds(0, SIZES[g]), pl.ds(0, TWO * QUART)]
+        send(got, got, w_s, w_r.at[g, side], peer).wait_recv()
 
     low_v = iota((QUART, S, S, L), TWO + 1) < N
 
-    def middle(p):
+    def middle(i0):
         for jo in range(TWO):
             rhs = jnp.concatenate(
-                [wbuf[p + H * s, jo * S:(jo + 1) * S].reshape(TWO * L, L) for s in range(TWO)], axis=1)
+                [wbuf[i0 + s, jo * S:(jo + 1) * S].reshape(TWO * L, L) for s in range(TWO)], axis=1)
             out = dot(l3[...], rhs)
             for s in range(TWO):
                 o = out[:, s * L:(s + 1) * L].reshape(QUART, S, TWO, S, L)
@@ -307,12 +328,23 @@
         for kb in range(QUART):
             out = dot(l2[...], jnp.concatenate([v3[kb, 0], v3[kb, 1]], axis=1))
             pair = jnp.concatenate([out[:, :L].reshape(N, S, L), out[:, L:].reshape(N, S, L)], axis=1)
-            v2_out[kb, :, pl.ds(pl.multiple_of(p * T, T), T), :] = pair.astype(BF16)
-
-    def all_middle(g):
-        @pl.loop(STARTS[g], STARTS[g] + SIZES[g])
-        def _(p):
-            middle(p)
+            v2_out[kb, :, pl.ds(pl.multiple_of(i0 * S, T), T), :] = pair.astype(BF16)
+
+    def near_middle(g):
+        @pl.loop(0, max(SIZES[g] // TWO, 1))
+        def _(n):
+            middle(y * H + STARTS[g] + TWO * n)
+
+    def far_middle(g):
+        @pl.loop(0, max(SIZES[g] // TWO, 1))
+        def _(n):
+            middle(oy * H + STARTS[g] + TWO * n)
+
+    def near_end(g):
+        gathered(g, SAME)
+
+    def far_end(g):
+        gathered(g, OTHER)
 
     def arrived(g):
         got = u1r.at[:, pl.ds(STARTS[g] * T, SIZES[g] * T)]
@@ -325,53 +357,87 @@
     send(cores, cores, d_sem.at[0], d_sem.at[1], peer).wait_recv()
     all_second(A)
     all_second(B)
-    third(A)
-    gather_first(A)
-    third(B)
-    gather_first(B)
-    depart(D)
     arrived(C)
     all_second(C)
-    forward(A)
-    forward(B)
+    third(A)
+    gather_near(A)
+    gather_far(A)
+    third(B)
+    gather_near(B)
+    gather_far(B)
+    depart(E)
     third(C)
-    gather_first(C)
-    depart(E)
+    gather_near(C)
+    gather_far(C)
+    depart(F)
     depart(G)
-    forward_diagonal(A)
-    gather_end(A)
-    all_middle(A)
-    forward_diagonal(B)
     arrived(D)
     all_second(D)
-    forward(C)
-    gather_end(B)
-    all_middle(B)
+    forward_near(A)
+    forward_far(A)
+    near_end(A)
+    near_middle(A)
+    forward_near(B)
+    forward_far(B)
+    near_end(B)
+    near_middle(B)
+    forward_near(C)
     third(D)
-    gather_first(D)
-    forward_diagonal(C)
+    gather_near(D)
+    gather_far(D)
+    forward_diagonal(A)
+    far_end(A)
+    far_middle(A)
+    forward_diagonal(B)
+    near_end(C)
+    near_middle(C)
     arrived(E)
     all_second(E)
-    gather_end(C)
-    all_middle(C)
+    forward_far(C)
+    forward_near(D)
+    far_end(B)
+    far_middle(B)
+    near_end(D)
+    near_middle(D)
+    arrived(F)
+    all_second(F)
     third(E)
-    gather_first(E)
+    gather_near(E)
+    gather_far(E)
+    forward_diagonal(C)
+    far_end(C)
+    far_middle(C)
+    third(F)
+    gather_near(F)
+    gather_far(F)
     arrived(G)
     all_second(G)
-    forward(D)
-    forward(E)
+    forward_near(E)
+    near_end(E)
+    near_middle(E)
+    forward_far(D)
+    forward_near(F)
+    forward_far(E)
     third(G)
-    gather_first(G)
+    gather_near(G)
+    gather_far(G)
     forward_diagonal(D)
+    forward_far(F)
     forward_diagonal(E)
-    gather_end(D)
-    all_middle(D)
-    forward(G)
+    far_end(D)
+    far_middle(D)
+    forward_near(G)
+    forward_diagonal(F)
+    forward_far(G)
     forward_diagonal(G)
-    gather_end(E)
-    all_middle(E)
-    gather_end(G)
-    all_middle(G)
+    near_end(F)
+    near_end(G)
+    near_middle(F)
+    far_end(E)
+    far_middle(E)
+    far_end(F)
+    far_end(G)
+    far_middle(F)
 
     sent = wbuf.at[pl.ds(0, KINDS * QUART), :]
     send(first, first, u1_sem.at[0], u1_sem.at[1], in_x).wait_send()
@@ -383,7 +449,7 @@
 
 def compress(x, a1, a2, a3, b1_t, b2_t, b3_t, d):
     vmem = pl.BlockSpec(memory_space=pltpu.VMEM)
-    hbm = pl.BlockSpec(memory_space=pl.ANY)
+    hbm = pl.BlockSpec(memory_space=pltpu.HBM)
     dma = pltpu.SemaphoreType.DMA
     u1 = pltpu.VMEM((N, H * T, L), BF16)
     spread = pltpu.VMEM((M * T, N * T), BF16)
@@ -391,9 +457,10 @@
     return pl.pallas_call(
         compress_body,
         out_shape=(pltpu.VMEM((QUART, N, M * S, L), BF16), pltpu.VMEM((N * S, M * S), BF16)),
-        in_specs=[hbm] + [vmem] * 7,
+        in_specs=[hbm] * 8,
         out_specs=(vmem, vmem),
         scratch_shapes=[
+            pltpu.VMEM((6, M, L), BF16), pltpu.VMEM((H, H, H), F32),
             pltpu.VMEM((NEAR, N, TWO, M, N), BF16), pltpu.VMEM((RING, N, TWO, M, N), BF16), u1, u1, u1,
             spread, spread, spread, spread, pltpu.VMEM((N, N), BF16),
             pltpu.VMEM((M * T, M * S), BF16), pltpu.VMEM((N * S, M * S), BF16),
@@ -401,7 +468,7 @@
             pltpu.VMEM((M, H, M, L), BF16), pltpu.VMEM((S, H, H * H), F32),
             pltpu.VMEM((QUART, TWO, M * S, L), BF16),
             dma((NEAR,)), dma((RING,)), dma((RING,)), pltpu.SemaphoreType.REGULAR,
-            dma((TWO,)), dma, dma((groups,)), dma, dma((groups,)), dma, dma((groups, QUART)), dma((TWO,)),
+            dma((TWO,)), dma, dma((groups,)), dma, dma((groups,)), dma, dma((groups, QUART + 1)), dma((TWO,)), dma((KINDS,)),
         ],
         compiler_params=pltpu.CompilerParams(collective_id=0, has_side_effects=True, vmem_limit_bytes=LIMIT),
         name="compress",

time: 162 us -> 161 us (level)
  no operation moved by 1% of the time
where the time goes in v5:
time: 161 us
  Pallas kernels  161 us (100%)
    pallas_call x1, Pallas kernels, compress(): pl.pallas_call(compress_body, out_shape=(pltpu.VMEM((QUART, N, M * S, L),...  119 us
    pallas_call x1, Pallas kernels, expand(): pl.pallas_call(expand_body, out_shape=jax.ShapeDtypeStruct((N, N, N, N),...  41.7 us

profile of v5, /device:TPU:0, one launch (start us, length us, event | category | flops | bytes accessed | tf_op | source)
XLA Modules:
  0.0 161.2 jit_solution(2093436291342241385)
XLA Ops:
  0.0 119.3 %compress.1 = (bf16[4,64,256,128]{3,2,1,0:T(8,128)(2,1)S(1)}, bf16[512,256]{1,0:T(8,128)(2,1)S(1)}) custom-call(bf16[64,64,64,64]{3,2,1,0:T(8,128)(2,1)} %x_hbm.1, bf16[32,128]{1,0:T(8,128)(2,1)} %a1_hbm.1, bf16[32,128]{1,0:T(8,128)(2,1)} %a2_hbm.1, bf16[32,128]{1,0:T(8,128)(2,1)} %a3_hbm.1, bf16[32,128]{1,0:T(8,128)(2,1)} %bitcast.3, ...), custom_call_target="tpu_custom_call" | custom-call | tf_op jit(solution)/shard_map/compress/pallas_call | solution.py:457
  119.3 41.7 %expand.1 = f32[64,64,64,64]{3,2,1,0:T(8,128)} custom-call(bf16[4,64,256,128]{3,2,1,0:T(8,128)(2,1)S(1)} %get-tuple-element.7.v2_ref, bf16[512,256]{1,0:T(8,128)(2,1)S(1)} %get-tuple-element.8.l1_ref), custom_call_target="tpu_custom_call" | custom-call | tf_op jit(solution)/shard_map/expand/pallas_call | solution.py:509

commit v6 on v5

--- a/solution.py
+++ b/solution.py
@@ -24,9 +24,9 @@
 A, B, C, D, E, F, G = range(7)
 SIZES = (4, 4, 2, 2, 2, 1, 1)
 STARTS = (0, 4, 8, 10, 12, 14, 15)
-CHUNKS = (0, 0, 4, 2, 2, 1, 1)
+CHUNKS = (0, 0, 8, 2, 2, 1, 1)
 DIRECT = (F, G)
-FILLERS = 2
+FILLERS = 4
 GROUPS = range(len(SIZES))
 OTHERS = range(1, QUART)
 DEVICES = range(1, S)
@@ -164,7 +164,7 @@
             early(t - 1).start()
 
         for n in range(FILLERS):
-            @pl.when(t == S * (n + 1) + 1)
+            @pl.when(t == QUART * (n + 1) + 1)
             def _(n=n):
                 late(C, n).start()
 

time: 161 us -> 161 us (level)
  no operation moved by 1% of the time
where the time goes in v6:
time: 161 us
  Pallas kernels  161 us (100%)
    pallas_call x1, Pallas kernels, compress(): pl.pallas_call(compress_body, out_shape=(pltpu.VMEM((QUART, N, M * S, L),...  119 us
    pallas_call x1, Pallas kernels, expand(): pl.pallas_call(expand_body, out_shape=jax.ShapeDtypeStruct((N, N, N, N),...  41.7 us

profile of v6, /device:TPU:0, one launch (start us, length us, event | category | flops | bytes accessed | tf_op | source)
XLA Modules:
  0.0 160.8 jit_solution(2099416065796840194)
XLA Ops:
  0.0 118.9 %compress.1 = (bf16[4,64,256,128]{3,2,1,0:T(8,128)(2,1)S(1)}, bf16[512,256]{1,0:T(8,128)(2,1)S(1)}) custom-call(bf16[64,64,64,64]{3,2,1,0:T(8,128)(2,1)} %x_hbm.1, bf16[32,128]{1,0:T(8,128)(2,1)} %a1_hbm.1, bf16[32,128]{1,0:T(8,128)(2,1)} %a2_hbm.1, bf16[32,128]{1,0:T(8,128)(2,1)} %a3_hbm.1, bf16[32,128]{1,0:T(8,128)(2,1)} %bitcast.3, ...), custom_call_target="tpu_custom_call" | custom-call | tf_op jit(solution)/shard_map/compress/pallas_call | solution.py:457
  118.9 41.7 %expand.1 = f32[64,64,64,64]{3,2,1,0:T(8,128)} custom-call(bf16[4,64,256,128]{3,2,1,0:T(8,128)(2,1)S(1)} %get-tuple-element.7.v2_ref, bf16[512,256]{1,0:T(8,128)(2,1)S(1)} %get-tuple-element.8.l1_ref), custom_call_target="tpu_custom_call" | custom-call | tf_op jit(solution)/shard_map/expand/pallas_call | solution.py:509

commit v7 on v6

--- a/solution.py
+++ b/solution.py
@@ -331,13 +331,11 @@
             v2_out[kb, :, pl.ds(pl.multiple_of(i0 * S, T), T), :] = pair.astype(BF16)
 
     def near_middle(g):
-        @pl.loop(0, max(SIZES[g] // TWO, 1))
-        def _(n):
+        for n in range(max(SIZES[g] // TWO, 1)):
             middle(y * H + STARTS[g] + TWO * n)
 
     def far_middle(g):
-        @pl.loop(0, max(SIZES[g] // TWO, 1))
-        def _(n):
+        for n in range(max(SIZES[g] // TWO, 1)):
             middle(oy * H + STARTS[g] + TWO * n)
 
     def near_end(g):

time: 161 us -> 161 us (level)
  no operation moved by 1% of the time
where the time goes in v7:
time: 161 us
  Pallas kernels  161 us (100%)
    pallas_call x1, Pallas kernels, compress(): pl.pallas_call(compress_body, out_shape=(pltpu.VMEM((QUART, N, M * S, L),...  119 us
    pallas_call x1, Pallas kernels, expand(): pl.pallas_call(expand_body, out_shape=jax.ShapeDtypeStruct((N, N, N, N),...  41.7 us

profile of v7, /device:TPU:0, one launch (start us, length us, event | category | flops | bytes accessed | tf_op | source)
XLA Modules:
  0.0 160.8 jit_solution(16808023155321902830)
XLA Ops:
  0.0 118.9 %compress.1 = (bf16[4,64,256,128]{3,2,1,0:T(8,128)(2,1)S(1)}, bf16[512,256]{1,0:T(8,128)(2,1)S(1)}) custom-call(bf16[64,64,64,64]{3,2,1,0:T(8,128)(2,1)} %x_hbm.1, bf16[32,128]{1,0:T(8,128)(2,1)} %a1_hbm.1, bf16[32,128]{1,0:T(8,128)(2,1)} %a2_hbm.1, bf16[32,128]{1,0:T(8,128)(2,1)} %a3_hbm.1, bf16[32,128]{1,0:T(8,128)(2,1)} %bitcast.3, ...), custom_call_target="tpu_custom_call" | custom-call | tf_op jit(solution)/shard_map/compress/pallas_call | solution.py:455
  118.9 41.7 %expand.1 = f32[64,64,64,64]{3,2,1,0:T(8,128)} custom-call(bf16[4,64,256,128]{3,2,1,0:T(8,128)(2,1)S(1)} %get-tuple-element.7.v2_ref, bf16[512,256]{1,0:T(8,128)(2,1)S(1)} %get-tuple-element.8.l1_ref), custom_call_target="tpu_custom_call" | custom-call | tf_op jit(solution)/shard_map/expand/pallas_call | solution.py:507
